TPU v7x, 32 devices: a whole 2x2x4 slice. The times are simulated.
32 devices in a mesh: dp: 2 (over x), sp: 4 (over z), uly: 4 (over y, core).
Axes of the slice: x: 2, y: 2, z: 4, core: 2. Of those that a mesh axis runs over, the one named last changes fastest.
Arguments:
- tokens: bfloat16 [2, 4096, 1536], P('dp', ('sp', 'uly')), parts along dimension 0
- rope_ang: float32 [4096, 64], P(('sp', 'uly'))
- t_emb: float32 [2, 6, 1536], P('dp'), parts along dimension 0
- block_mod: float32 [1, 6, 1536], replicated
- context: bfloat16 [2, 512, 1536], P('dp'), parts along dimension 0
- attn_wq: bfloat16 [1536, 1536], replicated
- attn_bq: bfloat16 [1536], replicated
- attn_wk: bfloat16 [1536, 1536], replicated
- attn_bk: bfloat16 [1536], replicated
- attn_wv: bfloat16 [1536, 1536], replicated
- attn_bv: bfloat16 [1536], replicated
- attn_gq: bfloat16 [1536], replicated
- attn_gk: bfloat16 [1536], replicated
- attn_wo: bfloat16 [1536, 1536], replicated
- attn_bo: bfloat16 [1536], replicated
- norm3_w: bfloat16 [1536], replicated
- norm3_b: bfloat16 [1536], replicated
- cross_wq: bfloat16 [1536, 1536], replicated
- cross_wk: bfloat16 [1536, 1536], replicated
- cross_wv: bfloat16 [1536, 1536], replicated
- cross_gq: bfloat16 [1536], replicated
- cross_gk: bfloat16 [1536], replicated
- cross_wo: bfloat16 [1536, 1536], replicated
- ffn_w1: bfloat16 [1536, 8960], replicated
- ffn_w2: bfloat16 [8960, 1536], replicated
Outputs:
- output: bfloat16 [2, 4096, 1536], P('dp', ('sp', 'uly')), parts along dimension 0
There are 2 independent parts. A program takes and returns all parts, laid end to end along the dimension named above; an argument that names none is the same for every part.
All inputs are finite; a program needn't handle non-finite values.
Results may differ from a plain program's by a relative error of at most 0.00550236.
Values are sent between devices in bfloat16 or wider.
A program may use at most 1 GiB of HBM per device.

v0:
```python
import math

import jax
import jax.numpy as jnp
from jax import lax
from jax.experimental import pallas as pl
from jax.experimental.pallas import tpu as pltpu
from jax.sharding import PartitionSpec as P

EPS = 1e-6
HEAD = 128
HEADS = 12
D = 1536
FF = 8960
TOK = 256
TEXT = 512
HALF = 768
DUAL = 32
AUX = 136
FT = 1280
RING = 4
MESH = pl.DeviceIdType.MESH
EXP_SCALE = math.log2(math.e) * HEAD ** -0.5
F32 = jnp.float32
BF16 = jnp.bfloat16
VMEM_MAX = 67043328


def dot(lhs, rhs):
    return jnp.dot(lhs, rhs, preferred_element_type=F32)


def dot_dims(lhs, rhs, l_dim, r_dim):
    return lax.dot_general(lhs, rhs, (((l_dim,), (r_dim,)), ((), ())), preferred_element_type=F32)


def swap_pairs(val):
    lane = lax.broadcasted_iota(jnp.int32, val.shape, 1)
    return jnp.where(lane % 2 == 0, pltpu.roll(val, 127, 1), pltpu.roll(val, 1, 1))


def over_pairs(cos_p, sin_p, base):
    lane = lax.broadcasted_iota(jnp.int32, (128, 128), 1)
    sign = jnp.where(lane % 2 == 0, -1.0, 1.0).astype(F32)
    pair = lane // 2 + base
    return jnp.take_along_axis(cos_p, pair, axis=1), jnp.take_along_axis(sin_p, pair, axis=1) * sign


def layer_norm_rows(x_f32):
    centered = x_f32 - jnp.mean(x_f32, axis=-1, keepdims=True)
    var = jnp.mean(centered * centered, axis=-1, keepdims=True)
    return centered * lax.rsqrt(var + EPS)


def fold_sq(val):
    return val[:, :128] * val[:, :128] + val[:, 128:] * val[:, 128:]


def inv_rms(ssq):
    return lax.rsqrt(jnp.sum(ssq, axis=1, keepdims=True) * (1.0 / D) + EPS)


def tile256(j):
    return pl.ds(pl.multiple_of(j * 256, 256), 256)


def tile128(j):
    return pl.ds(pl.multiple_of(j * 128, 128), 128)


def as_row(ref):
    return ref[...].astype(F32).reshape(1, D)


def attn_kernel(x_hbm, ang_hbm, c_hbm, wq_hbm, wk_hbm, wv_hbm, cwk_hbm, cwv_hbm,
                temb_ref, mod_ref, bq_ref, bk_ref, bv_ref, gq_ref, gk_ref, cgk_ref,
                o_hbm, ck_hbm, cvt_hbm,
                xbuf, ang, ctx, wq, wk, wv, cwk, cwv, vec,
                ybuf, abuf, raw, q_loc, q_got, q_t, k_b, v_b, cos_s, sin_s, cos_b, sin_b, inv_b, acc, m_s, l_s,
                craw, ck, cvt, ssq, obuf,
                rs, ss, loc, qo_s, qo_r):
    z = lax.axis_index('sp')
    u = lax.axis_index('uly')
    yy = u // 2
    cc = u % 2
    hi = z // 2
    zm = z * (1 - hi) + (3 - z) * hi
    UP, DN, YP, CP = 0, 1, 2, 3
    dev = ({'sp': (z + 1) % 4, 'uly': u}, {'sp': (z + 3) % 4, 'uly': u},
           {'sp': z, 'uly': (1 - yy) * 2 + cc}, {'sp': z, 'uly': yy * 2 + 1 - cc})
    ends = jnp.logical_or(z == 0, z == 3)
    mids = jnp.logical_and(z > 0, z < 3)

    def z_of(i):
        low = i // 2
        m_i = low * i + (1 - low) * (i + zm - 2 * i * zm)
        return m_i * (1 - hi) + (3 - m_i) * hi

    def slot_a(i):
        return z_of(i) * 4 + yy * 2 + cc

    def slot_b(i):
        return z_of(i) * 4 + (1 - yy) * 2 + cc

    def slot_c(i):
        return z_of(i) * 4 + yy * 2 + 1 - cc

    def slot_d(i):
        return z_of(i) * 4 + (1 - yy) * 2 + 1 - cc

    X1, X2, DU, M1, AX = 'x1', 'x2', 'du', 'm1', 'ax'
    rows_of = {X1: (0, 128), X2: (128, 128), DU: (0, DUAL), M1: (DUAL, 128 - DUAL)}
    sem_of = {X1: 0, M1: 0, X2: 1, DU: 2, AX: 3}

    def copy(slot, part, to):
        ref = abuf.at[slot] if part == AX else ybuf.at[slot, pl.ds(*rows_of[part])]
        key = sem_of[part]
        return pltpu.make_async_remote_copy(ref, ref, ss.at[to, key, slot], rs.at[key, slot], device_id=dev[to], device_id_type=MESH)

    def start(slot, to, *parts):
        for part in parts:
            copy(slot, part, to).start()

    def got(slot, *parts):
        for part in parts:
            copy(slot, part, CP).wait_recv()

    def sent(slot, to, *parts):
        for part in parts:
            copy(slot, part, to).wait_send()

    def along_z(act):
        @pl.when(z < 3)
        def _():
            act(UP)

        @pl.when(z > 0)
        def _():
            act(DN)

    def relay(i, act):
        to_1 = (UP, DN, DN)[i - 1]
        to_2 = (DN, UP, UP)[i - 1]

        @pl.when(z == 1)
        def _():
            act(to_1)

        @pl.when(z == 2)
        def _():
            act(to_2)

    barrier = pltpu.get_barrier_semaphore()
    for to in (YP, CP):
        pl.semaphore_signal(barrier, 1, device_id=dev[to], device_id_type=MESH)
    along_z(lambda to: pl.semaphore_signal(barrier, 1, device_id=dev[to], device_id_type=MESH))

    get_x = pltpu.make_async_copy(x_hbm.at[0], xbuf, loc.at[0])
    get_ang = pltpu.make_async_copy(ang_hbm, ang, loc.at[1])
    get_wk = pltpu.make_async_copy(wk_hbm, wk, loc.at[2])
    get_wq = pltpu.make_async_copy(wq_hbm, wq, loc.at[3])
    get_wv = pltpu.make_async_copy(wv_hbm.at[:, pl.ds(pl.multiple_of(cc * HALF, HALF), HALF)], wv, loc.at[4])
    get_ctx = pltpu.make_async_copy(c_hbm.at[0], ctx, loc.at[5])
    get_cwk = pltpu.make_async_copy(cwk_hbm, cwk, loc.at[6])
    get_cwv = pltpu.make_async_copy(cwv_hbm, cwv, loc.at[7])
    for get in (get_x, get_ang, get_wk, get_wq, get_wv, get_ctx, get_cwk, get_cwv):
        get.start()
    BQ, BK, BV, GQ, GK, CGK = range(6)
    for row, ref in enumerate((bq_ref, bk_ref, bv_ref, gq_ref, gk_ref, cgk_ref)):
        vec[row:row + 1] = as_row(ref)
    shift = temb_ref[0, 0:1] + mod_ref[0, 0:1]
    scale = 1.0 + (temb_ref[0, 1:2] + mod_ref[0, 1:2])
    mine = slot_a(0)
    get_x.wait()

    @pl.loop(0, TOK // 32)
    def _(part):
        rows = pl.ds(pl.multiple_of(part * 32, 32), 32)
        ybuf[mine, rows] = (layer_norm_rows(xbuf[rows].astype(F32)) * scale + shift).astype(BF16)

    @pl.when(ends)
    def _():
        pl.semaphore_wait(barrier, 3)

    @pl.when(mids)
    def _():
        pl.semaphore_wait(barrier, 4)

    start(mine, YP, DU, M1)
    along_z(lambda to: start(mine, to, X1))
    start(mine, CP, X1, X2)

    get_ang.wait()
    abuf[mine, 0:128] = jnp.concatenate([ang[0:128], ang[128:256]], axis=1)
    ssq[0] = jnp.zeros((TOK, 128), F32)
    ssq[1] = jnp.zeros((TOK, 128), F32)
    get_wk.wait()

    @pl.loop(0, 6)
    def _(j):
        ssq[0] += fold_sq(dot(ybuf[mine], wk[:, tile256(j)]) + vec[BK:BK + 1, tile256(j)])
    k_inv = inv_rms(ssq[0])
    for part in (0, 1):
        abuf[mine, 128 + part:129 + part] = jnp.broadcast_to(k_inv[part * 128:(part + 1) * 128], (128, 128)).T[0:1]
    abuf[mine, 130:136] = jnp.zeros((6, 128), F32)
    start(mine, YP, AX, X2)
    along_z(lambda to: start(mine, to, AX, X2))
    start(mine, CP, AX)

    get_wq.wait()

    @pl.loop(0, 6)
    def _(j):
        lin = dot(ybuf[mine], wq[:, tile256(j)]) + vec[BQ:BQ + 1, tile256(j)]
        raw[:, tile256(j)] = lin
        ssq[1] += fold_sq(lin)
    q_inv = inv_rms(ssq[1])
    packed = abuf[mine, 0:128]
    cos_p = jnp.cos(packed)
    sin_p = jnp.sin(packed)
    for part in (0, 1):
        rows = pl.ds(part * 128, 128)
        cos_d, sin_d = over_pairs(cos_p, sin_p, part * 64)
        for h in range(HEADS):
            cols = slice(h * 128, (h + 1) * 128)
            val = raw[rows, cols] * q_inv[part * 128:(part + 1) * 128] * vec[GQ:GQ + 1, cols]
            q_loc[h // 6, rows, (h % 6) * 128:(h % 6 + 1) * 128] = (val * cos_d + swap_pairs(val) * sin_d).astype(BF16)
    send_q = pltpu.make_async_remote_copy(q_loc.at[1 - cc], q_got, qo_s.at[0], qo_r.at[0], device_id=dev[CP], device_id_type=MESH)
    send_q.start()

    peer0 = slot_b(0)
    got(peer0, DU)
    along_z(lambda to: start(peer0, to, DU))
    start(peer0, CP, DU)

    def event_a(i, hf):
        slot = slot_a(i)
        peer = slot_b(i)
        if hf:
            got(slot, X2)
            relay(i, lambda to: start(slot, to, X2))
            start(slot, YP, X2)
            start(slot, CP, X2)
        else:
            got(slot, X1, AX)
            relay(i, lambda to: start(slot, to, X1, AX))
            start(slot, YP, M1, AX)
            start(slot, CP, X1, AX)
            got(peer, DU)
            relay(i, lambda to: start(peer, to, DU))
            start(peer, CP, DU)

    def event_b(i, hf):
        slot = slot_b(i)
        parts = (X2,) if hf else (M1, AX)
        got(slot, *parts)
        start(slot, CP, *parts)

    for h in range(6):
        cols = slice(h * 128, (h + 1) * 128)
        q_t[cols, pl.ds(pl.multiple_of(cc * TOK, TOK), TOK)] = q_loc[cc, :, cols].T
    acc[...] = jnp.zeros_like(acc)
    l_s[...] = jnp.zeros_like(l_s)
    m_s[...] = jnp.full_like(m_s, -jnp.inf)
    send_q.wait_recv()
    for h in range(6):
        cols = slice(h * 128, (h + 1) * 128)
        q_t[cols, pl.ds(pl.multiple_of((1 - cc) * TOK, TOK), TOK)] = q_got[:, cols].T
    get_wv.wait()

    def cross_k():
        get_ctx.wait()
        get_cwk.wait()
        ssq[...] = jnp.zeros_like(ssq)

        @pl.loop(0, 6)
        def _(j):
            lin = dot(ctx[...], cwk[:, tile256(j)])
            craw[:, tile256(j)] = lin
            sq = fold_sq(lin)
            ssq[0] += sq[:TOK]
            ssq[1] += sq[TOK:]
        inv_0 = inv_rms(ssq[0])
        inv_1 = inv_rms(ssq[1])

        @pl.loop(0, 6)
        def _(j):
            gain = vec[CGK:CGK + 1, tile256(j)]
            ck[0:TOK, tile256(j)] = (craw[0:TOK, tile256(j)] * inv_0 * gain).astype(BF16)
            ck[TOK:TEXT, tile256(j)] = (craw[TOK:TEXT, tile256(j)] * inv_1 * gain).astype(BF16)
        pltpu.make_async_copy(ck, ck_hbm, loc.at[8]).start()

    def cross_v():
        get_cwv.wait()

        @pl.loop(0, 6)
        def _(j):
            cvt[tile256(j), :] = dot(ctx[...], cwv[:, tile256(j)]).astype(BF16).T
        pltpu.make_async_copy(cvt, cvt_hbm, loc.at[9]).start()

    at_ends = {2: ('a', 1, 0), 4: ('a', 1, 1), 6: ('a', 2, 0), 8: ('a', 2, 1), 10: ('a', 3, 0), 12: ('a', 3, 1)}
    at_mids = {2: ('a', 1, 0, 2, 0), 4: ('a', 1, 1, 2, 1), 8: ('a', 3, 0), 10: ('a', 3, 1)}
    at_all = {3: (0, 0), 5: (0, 1), 7: (1, 0), 9: (1, 1), 11: (2, 0), 13: (2, 1), 14: (3, 0), 15: (3, 1)}

    def body(it, _):
        first = (15 - it) // 14
        last = it // 14
        mid = 1 - first - last
        r = (it + 2) % 4
        k = (it + 2) // 4 - 1
        is_bd = mid * (r % 2) + last
        hf = mid * (r // 2) + (first + last) * (it % 2)
        idx = mid * (k + 1 - r % 2) + last * 3

        for step in range(16):
            has_ends, has_mids, has_all = step in at_ends, step in at_mids, step in at_all
            if not (has_ends or has_mids or has_all):
                continue

            @pl.when(it == step)
            def _(step=step, has_ends=has_ends, has_mids=has_mids, has_all=has_all):
                if has_ends:
                    @pl.when(ends)
                    def _():
                        event_a(*at_ends[step][1:3])
                if has_mids:
                    @pl.when(mids)
                    def _():
                        todo = at_mids[step][1:]
                        for n in range(0, len(todo), 2):
                            event_a(todo[n], todo[n + 1])
                if has_all:
                    event_b(*at_all[step])

        pl.when(it == 4)(cross_k)
        pl.when(it == 8)(cross_v)

        @pl.when(jnp.logical_and(is_bd == 0, hf == 0))
        def _():
            got(slot_c(idx), X1, AX)

        @pl.when(jnp.logical_and(is_bd == 0, hf == 1))
        def _():
            got(slot_c(idx), X2)

        @pl.when(jnp.logical_and(is_bd == 1, hf == 0))
        def _():
            got(slot_d(idx), DU, M1, AX)

        @pl.when(jnp.logical_and(is_bd == 1, hf == 1))
        def _():
            got(slot_d(idx), X2)

        y_of = (1 - is_bd) * yy + is_bd * (1 - yy)
        base = z_of(idx) * 4 + y_of * 2

        @pl.when(hf == 0)
        def _():
            for s in (0, 1):
                packed = abuf[base + s, 0:128]
                cos_s[is_bd * 2 + s] = jnp.cos(packed)
                sin_s[is_bd * 2 + s] = jnp.sin(packed)
        for s in (0, 1):
            rows = slice(s * 128, (s + 1) * 128)
            cos_b[rows], sin_b[rows] = over_pairs(cos_s[is_bd * 2 + s], sin_s[is_bd * 2 + s], hf * 64)
            inv_b[rows] = jnp.broadcast_to(abuf[base + s, pl.ds(128 + hf, 1)], (128, 128)).T
        y_val = ybuf[pl.ds(base, 2), pl.ds(pl.multiple_of(hf * 128, 128), 128)].reshape(TOK, D)
        for hp in range(3):
            wide = slice(hp * 256, (hp + 1) * 256)
            mine_cols = pl.ds(pl.multiple_of(cc * HALF + hp * 256, 256), 256)
            k_lin = dot(y_val, wk[:, mine_cols]) + vec[BK:BK + 1, mine_cols]
            gain = vec[GK:GK + 1, mine_cols]
            for h2 in (0, 1):
                cols = slice(h2 * 128, (h2 + 1) * 128)
                val = k_lin[:, cols] * inv_b[...] * gain[:, cols]
                k_b[:, (hp * 2 + h2) * 128:(hp * 2 + h2 + 1) * 128] = (val * cos_b[...] + swap_pairs(val) * sin_b[...]).astype(BF16)
            v_b[:, wide] = (dot(y_val, wv[:, wide]) + vec[BV:BV + 1, mine_cols]).astype(BF16)
            for h2 in (0, 1):
                h = hp * 2 + h2
                cols = slice(h * 128, (h + 1) * 128)
                sc = dot(k_b[:, cols], q_t[cols])
                m_old = m_s[h]
                m_new = jnp.maximum(m_old, jnp.max(sc, axis=0, keepdims=True) * EXP_SCALE)
                w = jnp.exp2(sc * EXP_SCALE - m_new)
                alpha = jnp.exp2(m_old - m_new)
                l_s[h] = l_s[h] * alpha + jnp.sum(w, axis=0, keepdims=True)
                acc[h] = acc[h] * alpha + dot_dims(v_b[:, cols], w.astype(BF16), 0, 0)
                m_s[h] = m_new
        return 0

    lax.fori_loop(0, 16, body, 0)

    for h in range(6):
        cols = slice(h * 128, (h + 1) * 128)
        o_h = (acc[h] / l_s[h]).T.astype(BF16)
        obuf[0, :, cols] = o_h[:TOK]
        obuf[1, :, cols] = o_h[TOK:]
    send_o = pltpu.make_async_remote_copy(obuf.at[1 - cc], o_hbm.at[cc], qo_s.at[1], qo_r.at[1], device_id=dev[CP], device_id_type=MESH)
    got_o = pltpu.make_async_remote_copy(obuf.at[1 - cc], o_hbm.at[1 - cc], qo_s.at[1], qo_r.at[1], device_id=dev[CP], device_id_type=MESH)
    keep_o = pltpu.make_async_copy(obuf.at[cc], o_hbm.at[cc], loc.at[10])
    send_o.start()
    keep_o.start()

    sent(mine, YP, DU, M1, AX, X2)
    sent(mine, CP, X1, X2, AX)
    sent(peer0, CP, DU)

    def sent_z(to):
        sent(mine, to, X1, AX, X2)
        sent(peer0, to, DU)
    along_z(sent_z)
    for i in (1, 2, 3):
        slot = slot_a(i)
        peer = slot_b(i)

        def sent_on(to, slot=slot, peer=peer):
            sent(slot, to, X1, AX, X2)
            sent(peer, to, DU)
        relay(i, sent_on)
        sent(slot, YP, M1, AX, X2)
        sent(slot, CP, X1, AX, X2)
        sent(peer, CP, DU)
    for i in range(4):
        sent(slot_b(i), CP, M1, AX, X2)
    send_q.wait_send()
    pltpu.make_async_copy(ck, ck_hbm, loc.at[8]).wait()
    pltpu.make_async_copy(cvt, cvt_hbm, loc.at[9]).wait()
    send_o.wait_send()
    keep_o.wait()
    got_o.wait_recv()


def gather_attention(*args):
    any_spec = pl.BlockSpec(memory_space=pl.ANY)
    vmem_spec = pl.BlockSpec(memory_space=pltpu.VMEM)
    keys = 16 * TOK
    square = pltpu.VMEM((D, D), BF16)
    return pl.pallas_call(
        attn_kernel,
        out_shape=[jax.ShapeDtypeStruct((2, TOK, HALF), BF16), jax.ShapeDtypeStruct((TEXT, D), BF16), jax.ShapeDtypeStruct((D, TEXT), BF16)],
        in_specs=[any_spec] * 8 + [vmem_spec] * 8,
        out_specs=[any_spec] * 3,
        scratch_shapes=[
            pltpu.VMEM((TOK, D), BF16), pltpu.VMEM((TOK, 64), F32), pltpu.VMEM((TEXT, D), BF16),
            square, square, pltpu.VMEM((D, HALF), BF16), square, square, pltpu.VMEM((8, D), F32),
            pltpu.VMEM((16, TOK, D), BF16), pltpu.VMEM((16, AUX, 128), F32), pltpu.VMEM((TOK, D), F32),
            pltpu.VMEM((2, TOK, HALF), BF16), pltpu.VMEM((TOK, HALF), BF16), pltpu.VMEM((HALF, 2 * TOK), BF16),
            pltpu.VMEM((TOK, HALF), BF16), pltpu.VMEM((TOK, HALF), BF16),
            pltpu.VMEM((4, 128, 128), F32), pltpu.VMEM((4, 128, 128), F32),
            pltpu.VMEM((TOK, 128), F32), pltpu.VMEM((TOK, 128), F32), pltpu.VMEM((TOK, 128), F32),
            pltpu.VMEM((6, HEAD, 2 * TOK), F32), pltpu.VMEM((6, 1, 2 * TOK), F32), pltpu.VMEM((6, 1, 2 * TOK), F32),
            pltpu.VMEM((TEXT, D), F32), pltpu.VMEM((TEXT, D), BF16), pltpu.VMEM((D, TEXT), BF16), pltpu.VMEM((2, TOK, 128), F32),
            pltpu.VMEM((2, TOK, HALF), BF16),
            pltpu.SemaphoreType.DMA((4, 16)), pltpu.SemaphoreType.DMA((4, 4, 16)), pltpu.SemaphoreType.DMA((11,)),
            pltpu.SemaphoreType.DMA((2,)), pltpu.SemaphoreType.DMA((2,)),
        ],
        cost_estimate=pl.CostEstimate(flops=2 * keys * D * D + 4 * keys * HALF * 2 * TOK, bytes_accessed=10 * D * D, transcendentals=6 * keys * 2 * TOK),
        compiler_params=pltpu.CompilerParams(collective_id=0, has_side_effects=True, vmem_limit_bytes=VMEM_MAX),
        name="gather_attention",
    )(*args)


def tail_kernel(o_hbm, x_hbm, ck_hbm, cvt_hbm, wo_hbm, cwq_hbm, cwo_hbm, w1_hbm, w2_hbm,
                temb_ref, mod_ref, bo_ref, nw_ref, nb_ref, cgq_ref, out_ref,
                o_v, x_v, ck, cvt, wo, cwq, cwo, w1, w2, vec, res, lin, act, u_b, ssq, sems, ring):
    n_ff = FF // FT

    def ff_copies(t, slot):
        cols = pl.ds(pl.multiple_of(t * FT, FT), FT)
        return (pltpu.make_async_copy(w1_hbm.at[:, cols], w1.at[slot], ring.at[0, slot]),
                pltpu.make_async_copy(w2_hbm.at[cols], w2.at[slot], ring.at[1, slot]))

    gets = [pltpu.make_async_copy(src, dst, sems.at[n]) for n, (src, dst) in enumerate(
        ((o_hbm, o_v), (wo_hbm, wo), (x_hbm.at[0], x_v), (cwq_hbm, cwq), (ck_hbm, ck), (cvt_hbm, cvt), (cwo_hbm, cwo)))]
    for get in gets:
        get.start()
    for t in range(RING):
        for get in ff_copies(t, t):
            get.start()
    get_o, get_wo, get_x, get_cwq, get_ck, get_cvt, get_cwo = gets
    vec[0:6] = temb_ref[0] + mod_ref[0]
    BO, NW, NB, CGQ = 6, 7, 8, 9
    for row, ref in ((BO, bo_ref), (NW, nw_ref), (NB, nb_ref), (CGQ, cgq_ref)):
        vec[row:row + 1] = as_row(ref)

    get_o.wait()
    get_wo.wait()
    get_x.wait()

    @pl.loop(0, 6)
    def _(j):
        cols = tile256(j)
        prod = dot(o_v[0], wo[0:HALF, cols]) + dot(o_v[1], wo[HALF:D, cols])
        res[:, cols] = x_v[:, cols].astype(F32) + vec[2:3, cols] * (prod + vec[BO:BO + 1, cols])

    @pl.loop(0, TOK // 32)
    def _(part):
        rows = pl.ds(pl.multiple_of(part * 32, 32), 32)
        act[rows] = (layer_norm_rows(res[rows]) * vec[NW:NW + 1] + vec[NB:NB + 1]).astype(BF16)
    get_cwq.wait()
    ssq[...] = jnp.zeros_like(ssq)

    @pl.loop(0, 6)
    def _(j):
        prod = dot(act[...], cwq[:, tile256(j)])
        lin[:, tile256(j)] = prod
        ssq[...] += fold_sq(prod)
    q_inv = inv_rms(ssq[...])
    get_ck.wait()
    get_cvt.wait()

    @pl.loop(0, HEADS // 2)
    def _(hp):
        for h2 in (0, 1):
            cols = tile128(hp * 2 + h2)
            q_h = (lin[:, cols] * q_inv * vec[CGQ:CGQ + 1, cols]).astype(BF16)
            sc = dot_dims(ck[:, cols], q_h, 1, 1)
            m_row = jnp.max(sc, axis=0, keepdims=True) * EXP_SCALE
            w = jnp.exp2(sc * EXP_SCALE - m_row)
            o_t = dot(cvt[cols, :], w.astype(BF16)) / jnp.sum(w, axis=0, keepdims=True)
            act[:, cols] = o_t.T.astype(BF16)
    get_cwo.wait()

    @pl.loop(0, 6)
    def _(j):
        cols = tile256(j)
        res[:, cols] += dot(act[...], cwo[:, cols])

    @pl.loop(0, TOK // 32)
    def _(part):
        rows = pl.ds(pl.multiple_of(part * 32, 32), 32)
        act[rows] = (layer_norm_rows(res[rows]) * (1.0 + vec[4:5]) + vec[3:4]).astype(BF16)
        lin[rows] = jnp.zeros((32, D), F32)

    def ffn(t, _):
        slot = t % RING
        for get in ff_copies(t, slot):
            get.wait()
        for s in range(FT // 256):
            cols = slice(s * 256, (s + 1) * 256)
            u_b[:, cols] = jax.nn.gelu(dot(act[...], w1[slot, :, cols]), approximate=True).astype(BF16)
        for j in range(6):
            cols = slice(j * 256, (j + 1) * 256)
            lin[:, cols] += dot(u_b[...], w2[slot, :, cols])

        @pl.when(t + RING < n_ff)
        def _():
            for get in ff_copies(t + RING, slot):
                get.start()
        return 0

    lax.fori_loop(0, n_ff, ffn, 0)

    @pl.loop(0, TOK // 32)
    def _(part):
        rows = pl.ds(pl.multiple_of(part * 32, 32), 32)
        out_ref[0, rows] = (res[rows] + vec[5:6] * lin[rows]).astype(BF16)


def tail(*args):
    any_spec = pl.BlockSpec(memory_space=pl.ANY)
    vmem_spec = pl.BlockSpec(memory_space=pltpu.VMEM)
    square = pltpu.VMEM((D, D), BF16)
    return pl.pallas_call(
        tail_kernel,
        out_shape=jax.ShapeDtypeStruct((1, TOK, D), BF16),
        in_specs=[any_spec] * 9 + [vmem_spec] * 6,
        out_specs=vmem_spec,
        scratch_shapes=[
            pltpu.VMEM((2, TOK, HALF), BF16), pltpu.VMEM((TOK, D), BF16), pltpu.VMEM((TEXT, D), BF16), pltpu.VMEM((D, TEXT), BF16),
            square, square, square, pltpu.VMEM((RING, D, FT), BF16), pltpu.VMEM((RING, FT, D), BF16), pltpu.VMEM((16, D), F32),
            pltpu.VMEM((TOK, D), F32), pltpu.VMEM((TOK, D), F32), pltpu.VMEM((TOK, D), BF16), pltpu.VMEM((TOK, FT), BF16), pltpu.VMEM((TOK, 128), F32),
            pltpu.SemaphoreType.DMA((7,)), pltpu.SemaphoreType.DMA((2, RING)),
        ],
        cost_estimate=pl.CostEstimate(flops=4 * TOK * D * FF + 6 * TOK * D * D, bytes_accessed=4 * D * FF + 6 * D * D, transcendentals=TOK * FF),
        compiler_params=pltpu.CompilerParams(vmem_limit_bytes=VMEM_MAX),
        name="tail",
    )(*args)


def solution(mesh):
    tok_spec = P('dp', ('sp', 'uly'), None)
    batch_spec = P('dp', None, None)

    def local_block(tokens, rope_ang, t_emb, block_mod, context, attn_wq, attn_bq, attn_wk, attn_bk, attn_wv, attn_bv, attn_gq, attn_gk, attn_wo, attn_bo, norm3_w, norm3_b, cross_wq, cross_wk, cross_wv, cross_gq, cross_gk, cross_wo, ffn_w1, ffn_w2):
        o_half, cross_k, cross_vt = gather_attention(tokens, rope_ang, context, attn_wq, attn_wk, attn_wv, cross_wk, cross_wv, t_emb, block_mod, attn_bq, attn_bk, attn_bv, attn_gq, attn_gk, cross_gk)
        return tail(o_half, tokens, cross_k, cross_vt, attn_wo, cross_wq, cross_wo, ffn_w1, ffn_w2, t_emb, block_mod, attn_bo, norm3_w, norm3_b, cross_gq)

    in_specs = (tok_spec, P(('sp', 'uly'), None), batch_spec, P(), batch_spec) + (P(),) * 20
    return jax.shard_map(local_block, mesh=mesh, in_specs=in_specs, out_specs=tok_spec, check_vma=False)
```

profile of v0, /device:TPU:0, one launch (start us, length us, event | category | flops | bytes accessed | tf_op | source)
XLA Modules:
  0.0 169.1 jit_solution(3753265595930714512)
XLA Ops:
  0.0 1.4 copy.27.temb_ref
  1.4 1.4 copy.28.mod_ref
  2.8 1.6 copy.26.ang_hbm
  4.4 120.3 %gather_attention.1 = (bf16[2,256,768]{2,1,0:T(8,128)(2,1)}, bf16[512,1536]{1,0:T(8,128)(2,1)}, bf16[1536,512]{1,0:T(8,128)(2,1)}) custom-call(bf16[1,256,1536]{2,1,0:T(8,128)(2,1)} %x_hbm.3, f32[256,64]{1,0:T(8,128)} %copy.26.ang_hbm, bf16[1,512,1536]{2,1,0:T(8,128)(2,1)} %c_hbm.1, bf16[1536,1536]{1,0:T(8,128)(2,1)} %wq_hbm.1, bf16[1536,1536]{1,0:T(8,128)(2,1)} %wk_hbm.1, ...), custom_call_target="tpu_custom_call" | custom-call | flops 25769803776 | bytes 23592960 | tf_op jit(solution)/shard_map/gather_attention/pallas_call | solution.py:438
  124.7 44.4 %tail.1 = bf16[1,256,1536]{2,1,0:T(8,128)(2,1)} custom-call(bf16[2,256,768]{2,1,0:T(8,128)(2,1)} %get-tuple-element.8.o_hbm, bf16[1,256,1536]{2,1,0:T(8,128)(2,1)} %x_hbm.3, bf16[512,1536]{1,0:T(8,128)(2,1)} %get-tuple-element.9.ck_hbm, bf16[1536,512]{1,0:T(8,128)(2,1)} %get-tuple-element.10.cvt_hbm, bf16[1536,1536]{1,0:T(8,128)(2,1)} %wo_hbm.1, ...), custom_call_target="tpu_custom_call" | custom-call | flops 17716740096 | bytes 69206016 | tf_op jit(solution)/shard_map/tail/pallas_call | solution.py:564
where the time goes:
time: 169 us
  Pallas kernels  165 us (98%)
  local copies, waits for them, and re-layouts  4.37 us (3%)
    pallas_call x1, Pallas kernels, gather_attention(): pl.pallas_call(attn_kernel, out_shape=[jax.ShapeDtypeStruct((2, TOK, HALF...  120 us
    pallas_call x1, Pallas kernels, tail(): pl.pallas_call(tail_kernel, out_shape=jax.ShapeDtypeStruct((1, TOK, D), B...  44.4 us
    unnamed x3, local copies, waits for them, and re-layouts  4.37 us

commit v1 on v0

--- a/solution.py
+++ b/solution.py
@@ -9,10 +9,12 @@
 
 EPS = 1e-6
 HEAD = 128
+LANES = 128
 HEADS = 12
 D = 1536
 FF = 8960
 TOK = 256
+WIDE = 256
 TEXT = 512
 HALF = 768
 DUAL = 32
@@ -40,7 +42,7 @@
 
 
 def over_pairs(cos_p, sin_p, base):
-    lane = lax.broadcasted_iota(jnp.int32, (128, 128), 1)
+    lane = lax.broadcasted_iota(jnp.int32, (LANES, LANES), 1)
     sign = jnp.where(lane % 2 == 0, -1.0, 1.0).astype(F32)
     pair = lane // 2 + base
     return jnp.take_along_axis(cos_p, pair, axis=1), jnp.take_along_axis(sin_p, pair, axis=1) * sign
@@ -53,7 +55,7 @@
 
 
 def fold_sq(val):
-    return val[:, :128] * val[:, :128] + val[:, 128:] * val[:, 128:]
+    return val[:, :LANES] * val[:, :LANES] + val[:, LANES:] * val[:, LANES:]
 
 
 def inv_rms(ssq):
@@ -61,11 +63,16 @@
 
 
 def tile256(j):
-    return pl.ds(pl.multiple_of(j * 256, 256), 256)
+    return pl.ds(pl.multiple_of(j * WIDE, WIDE), WIDE)
 
 
 def tile128(j):
-    return pl.ds(pl.multiple_of(j * 128, 128), 128)
+    return pl.ds(pl.multiple_of(j * LANES, LANES), LANES)
+
+
+def ada_row(temb_ref, mod_ref, row):
+    cols = slice(row * D, (row + 1) * D)
+    return (temb_ref[cols] + mod_ref[cols]).reshape(1, D)
 
 
 def as_row(ref):
@@ -76,7 +83,7 @@
                 temb_ref, mod_ref, bq_ref, bk_ref, bv_ref, gq_ref, gk_ref, cgk_ref,
                 o_hbm, ck_hbm, cvt_hbm,
                 xbuf, ang, ctx, wq, wk, wv, cwk, cwv, vec,
-                ybuf, abuf, raw, q_loc, q_got, q_t, k_b, v_b, cos_s, sin_s, cos_b, sin_b, inv_b, acc, m_s, l_s,
+                ybuf, abuf, raw, q_loc, q_got, q_t, k_b, v_b, cos_s, sin_s, cos_b, sin_b, inv_b, acc, m_s, l_s, k_f, sc_s, w_s,
                 craw, ck, cvt, ssq, obuf,
                 rs, ss, loc, qo_s, qo_r):
     z = lax.axis_index('sp')
@@ -109,7 +116,7 @@
         return z_of(i) * 4 + (1 - yy) * 2 + 1 - cc
 
     X1, X2, DU, M1, AX = 'x1', 'x2', 'du', 'm1', 'ax'
-    rows_of = {X1: (0, 128), X2: (128, 128), DU: (0, DUAL), M1: (DUAL, 128 - DUAL)}
+    rows_of = {X1: (0, LANES), X2: (LANES, LANES), DU: (0, DUAL), M1: (DUAL, LANES - DUAL)}
     sem_of = {X1: 0, M1: 0, X2: 1, DU: 2, AX: 3}
 
     def copy(slot, part, to):
@@ -163,15 +170,16 @@
     get_ctx = pltpu.make_async_copy(c_hbm.at[0], ctx, loc.at[5])
     get_cwk = pltpu.make_async_copy(cwk_hbm, cwk, loc.at[6])
     get_cwv = pltpu.make_async_copy(cwv_hbm, cwv, loc.at[7])
-    for get in (get_x, get_ang, get_wk, get_wq, get_wv, get_ctx, get_cwk, get_cwv):
+    for get in (get_x, get_ang, get_wk):
         get.start()
     BQ, BK, BV, GQ, GK, CGK = range(6)
     for row, ref in enumerate((bq_ref, bk_ref, bv_ref, gq_ref, gk_ref, cgk_ref)):
         vec[row:row + 1] = as_row(ref)
-    shift = temb_ref[0, 0:1] + mod_ref[0, 0:1]
-    scale = 1.0 + (temb_ref[0, 1:2] + mod_ref[0, 1:2])
+    shift = ada_row(temb_ref, mod_ref, 0)
+    scale = 1.0 + ada_row(temb_ref, mod_ref, 1)
     mine = slot_a(0)
     get_x.wait()
+    get_wq.start()
 
     @pl.loop(0, TOK // 32)
     def _(part):
@@ -191,18 +199,20 @@
     start(mine, CP, X1, X2)
 
     get_ang.wait()
-    abuf[mine, 0:128] = jnp.concatenate([ang[0:128], ang[128:256]], axis=1)
-    ssq[0] = jnp.zeros((TOK, 128), F32)
-    ssq[1] = jnp.zeros((TOK, 128), F32)
+    abuf[mine, 0:LANES] = jnp.concatenate([ang[:, 0:LANES], ang[:, LANES:WIDE]], axis=0).T
+    ssq[0] = jnp.zeros((TOK, LANES), F32)
+    ssq[1] = jnp.zeros((TOK, LANES), F32)
     get_wk.wait()
+    for get in (get_wv, get_ctx, get_cwk, get_cwv):
+        get.start()
 
     @pl.loop(0, 6)
     def _(j):
         ssq[0] += fold_sq(dot(ybuf[mine], wk[:, tile256(j)]) + vec[BK:BK + 1, tile256(j)])
     k_inv = inv_rms(ssq[0])
     for part in (0, 1):
-        abuf[mine, 128 + part:129 + part] = jnp.broadcast_to(k_inv[part * 128:(part + 1) * 128], (128, 128)).T[0:1]
-    abuf[mine, 130:136] = jnp.zeros((6, 128), F32)
+        abuf[mine, LANES + part:129 + part] = jnp.broadcast_to(k_inv[part * LANES:(part + 1) * LANES], (LANES, LANES)).T[0:1]
+    abuf[mine, 130:136] = jnp.zeros((6, LANES), F32)
     start(mine, YP, AX, X2)
     along_z(lambda to: start(mine, to, AX, X2))
     start(mine, CP, AX)
@@ -215,16 +225,16 @@
         raw[:, tile256(j)] = lin
         ssq[1] += fold_sq(lin)
     q_inv = inv_rms(ssq[1])
-    packed = abuf[mine, 0:128]
+    packed = abuf[mine, 0:LANES]
     cos_p = jnp.cos(packed)
     sin_p = jnp.sin(packed)
     for part in (0, 1):
-        rows = pl.ds(part * 128, 128)
+        rows = pl.ds(part * LANES, LANES)
         cos_d, sin_d = over_pairs(cos_p, sin_p, part * 64)
         for h in range(HEADS):
-            cols = slice(h * 128, (h + 1) * 128)
-            val = raw[rows, cols] * q_inv[part * 128:(part + 1) * 128] * vec[GQ:GQ + 1, cols]
-            q_loc[h // 6, rows, (h % 6) * 128:(h % 6 + 1) * 128] = (val * cos_d + swap_pairs(val) * sin_d).astype(BF16)
+            cols = slice(h * LANES, (h + 1) * LANES)
+            val = raw[rows, cols] * q_inv[part * LANES:(part + 1) * LANES] * vec[GQ:GQ + 1, cols]
+            q_loc[h // 6, rows, (h % 6) * LANES:(h % 6 + 1) * LANES] = (val * cos_d + swap_pairs(val) * sin_d).astype(BF16)
     send_q = pltpu.make_async_remote_copy(q_loc.at[1 - cc], q_got, qo_s.at[0], qo_r.at[0], device_id=dev[CP], device_id_type=MESH)
     send_q.start()
 
@@ -257,14 +267,14 @@
         start(slot, CP, *parts)
 
     for h in range(6):
-        cols = slice(h * 128, (h + 1) * 128)
+        cols = slice(h * LANES, (h + 1) * LANES)
         q_t[cols, pl.ds(pl.multiple_of(cc * TOK, TOK), TOK)] = q_loc[cc, :, cols].T
     acc[...] = jnp.zeros_like(acc)
     l_s[...] = jnp.zeros_like(l_s)
     m_s[...] = jnp.full_like(m_s, -jnp.inf)
     send_q.wait_recv()
     for h in range(6):
-        cols = slice(h * 128, (h + 1) * 128)
+        cols = slice(h * LANES, (h + 1) * LANES)
         q_t[cols, pl.ds(pl.multiple_of((1 - cc) * TOK, TOK), TOK)] = q_got[:, cols].T
     get_wv.wait()
 
@@ -357,42 +367,66 @@
         @pl.when(hf == 0)
         def _():
             for s in (0, 1):
-                packed = abuf[base + s, 0:128]
+                packed = abuf[base + s, 0:LANES]
                 cos_s[is_bd * 2 + s] = jnp.cos(packed)
                 sin_s[is_bd * 2 + s] = jnp.sin(packed)
         for s in (0, 1):
-            rows = slice(s * 128, (s + 1) * 128)
+            rows = slice(s * LANES, (s + 1) * LANES)
             cos_b[rows], sin_b[rows] = over_pairs(cos_s[is_bd * 2 + s], sin_s[is_bd * 2 + s], hf * 64)
-            inv_b[rows] = jnp.broadcast_to(abuf[base + s, pl.ds(128 + hf, 1)], (128, 128)).T
-        y_val = ybuf[pl.ds(base, 2), pl.ds(pl.multiple_of(hf * 128, 128), 128)].reshape(TOK, D)
+            inv_b[rows] = jnp.broadcast_to(abuf[base + s, pl.ds(LANES + hf, 1)], (LANES, LANES)).T
+        y_val = ybuf[pl.ds(base, 2), pl.ds(pl.multiple_of(hf * LANES, LANES), LANES)].reshape(TOK, D)
+
+        def k_dot(hp):
+            cols = pl.ds(pl.multiple_of(cc * HALF + hp * WIDE, WIDE), WIDE)
+            k_f[:, hp * WIDE:(hp + 1) * WIDE] = dot(y_val, wk[:, cols])
+
+        def k_rope(h):
+            cols = pl.ds(pl.multiple_of(cc * HALF + h * LANES, LANES), LANES)
+            val = (k_f[:, h * LANES:(h + 1) * LANES] + vec[BK:BK + 1, cols]) * inv_b[...] * vec[GK:GK + 1, cols]
+            k_b[:, h * LANES:(h + 1) * LANES] = (val * cos_b[...] + swap_pairs(val) * sin_b[...]).astype(BF16)
+
+        def v_dot(hp):
+            cols = pl.ds(pl.multiple_of(cc * HALF + hp * WIDE, WIDE), WIDE)
+            wide = slice(hp * WIDE, (hp + 1) * WIDE)
+            v_b[:, wide] = (dot(y_val, wv[:, wide]) + vec[BV:BV + 1, cols]).astype(BF16)
+
+        def score(h):
+            cols = slice(h * LANES, (h + 1) * LANES)
+            sc = dot(k_b[:, cols], q_t[cols])
+            sc_s[h % 3] = sc
+            m_old = m_s[h]
+            m_new = jnp.maximum(m_old, jnp.max(sc, axis=0, keepdims=True) * EXP_SCALE)
+            m_s[h] = m_new
+            return m_new, jnp.exp2(m_old - m_new)
+
+        def weigh(h, m_new, alpha):
+            w = jnp.exp2(sc_s[h % 3] * EXP_SCALE - m_new)
+            l_s[h] = l_s[h] * alpha + jnp.sum(w.reshape(32, 8, 2 * TOK), axis=0)
+            w_s[h % 2] = w.astype(BF16)
+
+        def add_up(h, alpha):
+            cols = slice(h * LANES, (h + 1) * LANES)
+            acc[h] = acc[h] * alpha + dot_dims(v_b[:, cols], w_s[h % 2], 0, 0)
+
         for hp in range(3):
-            wide = slice(hp * 256, (hp + 1) * 256)
-            mine_cols = pl.ds(pl.multiple_of(cc * HALF + hp * 256, 256), 256)
-            k_lin = dot(y_val, wk[:, mine_cols]) + vec[BK:BK + 1, mine_cols]
-            gain = vec[GK:GK + 1, mine_cols]
-            for h2 in (0, 1):
-                cols = slice(h2 * 128, (h2 + 1) * 128)
-                val = k_lin[:, cols] * inv_b[...] * gain[:, cols]
-                k_b[:, (hp * 2 + h2) * 128:(hp * 2 + h2 + 1) * 128] = (val * cos_b[...] + swap_pairs(val) * sin_b[...]).astype(BF16)
-            v_b[:, wide] = (dot(y_val, wv[:, wide]) + vec[BV:BV + 1, mine_cols]).astype(BF16)
-            for h2 in (0, 1):
-                h = hp * 2 + h2
-                cols = slice(h * 128, (h + 1) * 128)
-                sc = dot(k_b[:, cols], q_t[cols])
-                m_old = m_s[h]
-                m_new = jnp.maximum(m_old, jnp.max(sc, axis=0, keepdims=True) * EXP_SCALE)
-                w = jnp.exp2(sc * EXP_SCALE - m_new)
-                alpha = jnp.exp2(m_old - m_new)
-                l_s[h] = l_s[h] * alpha + jnp.sum(w, axis=0, keepdims=True)
-                acc[h] = acc[h] * alpha + dot_dims(v_b[:, cols], w.astype(BF16), 0, 0)
-                m_s[h] = m_new
+            k_dot(hp)
+        for hp in range(3):
+            v_dot(hp)
+        for h in range(6):
+            k_rope(h)
+        st = {0: score(0), 1: score(1)}
+        for h in range(6):
+            weigh(h, *st[h])
+            if h + 2 < 6:
+                st[h + 2] = score(h + 2)
+            add_up(h, st[h][1])
         return 0
 
     lax.fori_loop(0, 16, body, 0)
 
     for h in range(6):
-        cols = slice(h * 128, (h + 1) * 128)
-        o_h = (acc[h] / l_s[h]).T.astype(BF16)
+        cols = slice(h * LANES, (h + 1) * LANES)
+        o_h = (acc[h] / jnp.sum(l_s[h], axis=0, keepdims=True)).T.astype(BF16)
         obuf[0, :, cols] = o_h[:TOK]
         obuf[1, :, cols] = o_h[TOK:]
     send_o = pltpu.make_async_remote_copy(obuf.at[1 - cc], o_hbm.at[cc], qo_s.at[1], qo_r.at[1], device_id=dev[CP], device_id_type=MESH)
@@ -441,15 +475,16 @@
         in_specs=[any_spec] * 8 + [vmem_spec] * 8,
         out_specs=[any_spec] * 3,
         scratch_shapes=[
-            pltpu.VMEM((TOK, D), BF16), pltpu.VMEM((TOK, 64), F32), pltpu.VMEM((TEXT, D), BF16),
+            pltpu.VMEM((TOK, D), BF16), pltpu.VMEM((HEAD // 2, TOK), F32), pltpu.VMEM((TEXT, D), BF16),
             square, square, pltpu.VMEM((D, HALF), BF16), square, square, pltpu.VMEM((8, D), F32),
-            pltpu.VMEM((16, TOK, D), BF16), pltpu.VMEM((16, AUX, 128), F32), pltpu.VMEM((TOK, D), F32),
+            pltpu.VMEM((16, TOK, D), BF16), pltpu.VMEM((16, AUX, LANES), F32), pltpu.VMEM((TOK, D), F32),
             pltpu.VMEM((2, TOK, HALF), BF16), pltpu.VMEM((TOK, HALF), BF16), pltpu.VMEM((HALF, 2 * TOK), BF16),
             pltpu.VMEM((TOK, HALF), BF16), pltpu.VMEM((TOK, HALF), BF16),
-            pltpu.VMEM((4, 128, 128), F32), pltpu.VMEM((4, 128, 128), F32),
-            pltpu.VMEM((TOK, 128), F32), pltpu.VMEM((TOK, 128), F32), pltpu.VMEM((TOK, 128), F32),
-            pltpu.VMEM((6, HEAD, 2 * TOK), F32), pltpu.VMEM((6, 1, 2 * TOK), F32), pltpu.VMEM((6, 1, 2 * TOK), F32),
-            pltpu.VMEM((TEXT, D), F32), pltpu.VMEM((TEXT, D), BF16), pltpu.VMEM((D, TEXT), BF16), pltpu.VMEM((2, TOK, 128), F32),
+            pltpu.VMEM((4, LANES, LANES), F32), pltpu.VMEM((4, LANES, LANES), F32),
+            pltpu.VMEM((TOK, LANES), F32), pltpu.VMEM((TOK, LANES), F32), pltpu.VMEM((TOK, LANES), F32),
+            pltpu.VMEM((6, HEAD, 2 * TOK), F32), pltpu.VMEM((6, 1, 2 * TOK), F32), pltpu.VMEM((6, 8, 2 * TOK), F32),
+            pltpu.VMEM((TOK, HALF), F32), pltpu.VMEM((3, TOK, 2 * TOK), F32), pltpu.VMEM((2, TOK, 2 * TOK), BF16),
+            pltpu.VMEM((TEXT, D), F32), pltpu.VMEM((TEXT, D), BF16), pltpu.VMEM((D, TEXT), BF16), pltpu.VMEM((2, TOK, LANES), F32),
             pltpu.VMEM((2, TOK, HALF), BF16),
             pltpu.SemaphoreType.DMA((4, 16)), pltpu.SemaphoreType.DMA((4, 4, 16)), pltpu.SemaphoreType.DMA((11,)),
             pltpu.SemaphoreType.DMA((2,)), pltpu.SemaphoreType.DMA((2,)),
@@ -472,19 +507,19 @@
 
     gets = [pltpu.make_async_copy(src, dst, sems.at[n]) for n, (src, dst) in enumerate(
         ((o_hbm, o_v), (wo_hbm, wo), (x_hbm.at[0], x_v), (cwq_hbm, cwq), (ck_hbm, ck), (cvt_hbm, cvt), (cwo_hbm, cwo)))]
-    for get in gets:
+    get_o, get_wo, get_x, get_cwq, get_ck, get_cvt, get_cwo = gets
+    for get in (get_o, get_wo, get_x, get_cwq):
         get.start()
-    for t in range(RING):
-        for get in ff_copies(t, t):
-            get.start()
-    get_o, get_wo, get_x, get_cwq, get_ck, get_cvt, get_cwo = gets
-    vec[0:6] = temb_ref[0] + mod_ref[0]
+    for row in range(6):
+        vec[row:row + 1] = ada_row(temb_ref, mod_ref, row)
     BO, NW, NB, CGQ = 6, 7, 8, 9
     for row, ref in ((BO, bo_ref), (NW, nw_ref), (NB, nb_ref), (CGQ, cgq_ref)):
         vec[row:row + 1] = as_row(ref)
 
     get_o.wait()
     get_wo.wait()
+    for get in (get_ck, get_cvt, get_cwo):
+        get.start()
     get_x.wait()
 
     @pl.loop(0, 6)
@@ -498,6 +533,9 @@
         rows = pl.ds(pl.multiple_of(part * 32, 32), 32)
         act[rows] = (layer_norm_rows(res[rows]) * vec[NW:NW + 1] + vec[NB:NB + 1]).astype(BF16)
     get_cwq.wait()
+    for t in range(RING):
+        for get in ff_copies(t, t):
+            get.start()
     ssq[...] = jnp.zeros_like(ssq)
 
     @pl.loop(0, 6)
@@ -536,11 +574,11 @@
         slot = t % RING
         for get in ff_copies(t, slot):
             get.wait()
-        for s in range(FT // 256):
-            cols = slice(s * 256, (s + 1) * 256)
+        for s in range(FT // WIDE):
+            cols = slice(s * WIDE, (s + 1) * WIDE)
             u_b[:, cols] = jax.nn.gelu(dot(act[...], w1[slot, :, cols]), approximate=True).astype(BF16)
         for j in range(6):
-            cols = slice(j * 256, (j + 1) * 256)
+            cols = slice(j * WIDE, (j + 1) * WIDE)
             lin[:, cols] += dot(u_b[...], w2[slot, :, cols])
 
         @pl.when(t + RING < n_ff)
@@ -569,7 +607,7 @@
         scratch_shapes=[
             pltpu.VMEM((2, TOK, HALF), BF16), pltpu.VMEM((TOK, D), BF16), pltpu.VMEM((TEXT, D), BF16), pltpu.VMEM((D, TEXT), BF16),
             square, square, square, pltpu.VMEM((RING, D, FT), BF16), pltpu.VMEM((RING, FT, D), BF16), pltpu.VMEM((16, D), F32),
-            pltpu.VMEM((TOK, D), F32), pltpu.VMEM((TOK, D), F32), pltpu.VMEM((TOK, D), BF16), pltpu.VMEM((TOK, FT), BF16), pltpu.VMEM((TOK, 128), F32),
+            pltpu.VMEM((TOK, D), F32), pltpu.VMEM((TOK, D), F32), pltpu.VMEM((TOK, D), BF16), pltpu.VMEM((TOK, FT), BF16), pltpu.VMEM((TOK, LANES), F32),
             pltpu.SemaphoreType.DMA((7,)), pltpu.SemaphoreType.DMA((2, RING)),
         ],
         cost_estimate=pl.CostEstimate(flops=4 * TOK * D * FF + 6 * TOK * D * D, bytes_accessed=4 * D * FF + 6 * D * D, transcendentals=TOK * FF),
@@ -583,8 +621,8 @@
     batch_spec = P('dp', None, None)
 
     def local_block(tokens, rope_ang, t_emb, block_mod, context, attn_wq, attn_bq, attn_wk, attn_bk, attn_wv, attn_bv, attn_gq, attn_gk, attn_wo, attn_bo, norm3_w, norm3_b, cross_wq, cross_wk, cross_wv, cross_gq, cross_gk, cross_wo, ffn_w1, ffn_w2):
-        o_half, cross_k, cross_vt = gather_attention(tokens, rope_ang, context, attn_wq, attn_wk, attn_wv, cross_wk, cross_wv, t_emb, block_mod, attn_bq, attn_bk, attn_bv, attn_gq, attn_gk, cross_gk)
-        return tail(o_half, tokens, cross_k, cross_vt, attn_wo, cross_wq, cross_wo, ffn_w1, ffn_w2, t_emb, block_mod, attn_bo, norm3_w, norm3_b, cross_gq)
+        o_half, cross_k, cross_vt = gather_attention(tokens, rope_ang.T, context, attn_wq, attn_wk, attn_wv, cross_wk, cross_wv, t_emb.reshape(-1), block_mod.reshape(-1), attn_bq, attn_bk, attn_bv, attn_gq, attn_gk, cross_gk)
+        return tail(o_half, tokens, cross_k, cross_vt, attn_wo, cross_wq, cross_wo, ffn_w1, ffn_w2, t_emb.reshape(-1), block_mod.reshape(-1), attn_bo, norm3_w, norm3_b, cross_gq)
 
     in_specs = (tok_spec, P(('sp', 'uly'), None), batch_spec, P(), batch_spec) + (P(),) * 20
     return jax.shard_map(local_block, mesh=mesh, in_specs=in_specs, out_specs=tok_spec, check_vma=False)

time: 169 us -> 143 us (0.85)
  Pallas kernels: 165 us -> 142 us
  local copies, waits for them, and re-layouts: 4.37 us -> 0 us
    pallas_call x1, Pallas kernels: 120 us -> 102 us  [gather_attention(): pl.pallas_call(attn_kernel, out_shape=[jax.ShapeDtypeStruct((2, TOK, HALF...]
    unnamed x3 -> x0, local copies, waits for them, and re-layouts: 4.37 us -> none
    pallas_call x1, Pallas kernels: 44.4 us -> 40.8 us  [tail(): pl.pallas_call(tail_kernel, out_shape=jax.ShapeDtypeStruct((1, TOK, D), B...]
where the time goes in v1:
time: 143 us; the launch traced here: 142 us
  Pallas kernels  142 us (99%)
    pallas_call x1, Pallas kernels, gather_attention(): pl.pallas_call(attn_kernel, out_shape=[jax.ShapeDtypeStruct((2, TOK, HALF...  102 us
    pallas_call x1, Pallas kernels, tail(): pl.pallas_call(tail_kernel, out_shape=jax.ShapeDtypeStruct((1, TOK, D), B...  40.8 us

profile of v1, /device:TPU:0, one launch (start us, length us, event | category | flops | bytes accessed | tf_op | source)
XLA Modules:
  0.0 142.4 jit_solution(11915889790054003198)
XLA Ops:
  0.0 101.6 %gather_attention.1 = (bf16[2,256,768]{2,1,0:T(8,128)(2,1)}, bf16[512,1536]{1,0:T(8,128)(2,1)}, bf16[1536,512]{1,0:T(8,128)(2,1)}) custom-call(bf16[1,256,1536]{2,1,0:T(8,128)(2,1)} %x_hbm.3, f32[64,256]{1,0:T(8,128)} %bitcast.7, bf16[1,512,1536]{2,1,0:T(8,128)(2,1)} %c_hbm.1, bf16[1536,1536]{1,0:T(8,128)(2,1)} %wq_hbm.1, bf16[1536,1536]{1,0:T(8,128)(2,1)} %wk_hbm.1, ...), custom_call_target="tpu_custom_call" | custom-call | flops 25769803776 | bytes 23592960 | tf_op jit(solution)/shard_map/gather_attention/pallas_call | solution.py:472
  101.6 40.8 %tail.1 = bf16[1,256,1536]{2,1,0:T(8,128)(2,1)} custom-call(bf16[2,256,768]{2,1,0:T(8,128)(2,1)} %get-tuple-element.8.o_hbm, bf16[1,256,1536]{2,1,0:T(8,128)(2,1)} %x_hbm.3, bf16[512,1536]{1,0:T(8,128)(2,1)} %get-tuple-element.9.ck_hbm, bf16[1536,512]{1,0:T(8,128)(2,1)} %get-tuple-element.10.cvt_hbm, bf16[1536,1536]{1,0:T(8,128)(2,1)} %wo_hbm.1, ...), custom_call_target="tpu_custom_call" | custom-call | flops 17716740096 | bytes 69206016 | tf_op jit(solution)/shard_map/tail/pallas_call | solution.py:602

commit v2 on v1

--- a/solution.py
+++ b/solution.py
@@ -63,11 +63,7 @@
 
 
 def tile256(j):
-    return pl.ds(pl.multiple_of(j * WIDE, WIDE), WIDE)
-
-
-def tile128(j):
-    return pl.ds(pl.multiple_of(j * LANES, LANES), LANES)
+    return slice(j * WIDE, (j + 1) * WIDE)
 
 
 def ada_row(temb_ref, mod_ref, row):
@@ -181,9 +177,8 @@
     get_x.wait()
     get_wq.start()
 
-    @pl.loop(0, TOK // 32)
-    def _(part):
-        rows = pl.ds(pl.multiple_of(part * 32, 32), 32)
+    for part in range(TOK // 32):
+        rows = slice(part * 32, (part + 1) * 32)
         ybuf[mine, rows] = (layer_norm_rows(xbuf[rows].astype(F32)) * scale + shift).astype(BF16)
 
     @pl.when(ends)
@@ -206,8 +201,7 @@
     for get in (get_wv, get_ctx, get_cwk, get_cwv):
         get.start()
 
-    @pl.loop(0, 6)
-    def _(j):
+    for j in range(6):
         ssq[0] += fold_sq(dot(ybuf[mine], wk[:, tile256(j)]) + vec[BK:BK + 1, tile256(j)])
     k_inv = inv_rms(ssq[0])
     for part in (0, 1):
@@ -219,8 +213,7 @@
 
     get_wq.wait()
 
-    @pl.loop(0, 6)
-    def _(j):
+    for j in range(6):
         lin = dot(ybuf[mine], wq[:, tile256(j)]) + vec[BQ:BQ + 1, tile256(j)]
         raw[:, tile256(j)] = lin
         ssq[1] += fold_sq(lin)
@@ -283,8 +276,7 @@
         get_cwk.wait()
         ssq[...] = jnp.zeros_like(ssq)
 
-        @pl.loop(0, 6)
-        def _(j):
+        for j in range(6):
             lin = dot(ctx[...], cwk[:, tile256(j)])
             craw[:, tile256(j)] = lin
             sq = fold_sq(lin)
@@ -293,8 +285,7 @@
         inv_0 = inv_rms(ssq[0])
         inv_1 = inv_rms(ssq[1])
 
-        @pl.loop(0, 6)
-        def _(j):
+        for j in range(6):
             gain = vec[CGK:CGK + 1, tile256(j)]
             ck[0:TOK, tile256(j)] = (craw[0:TOK, tile256(j)] * inv_0 * gain).astype(BF16)
             ck[TOK:TEXT, tile256(j)] = (craw[TOK:TEXT, tile256(j)] * inv_1 * gain).astype(BF16)
@@ -303,8 +294,7 @@
     def cross_v():
         get_cwv.wait()
 
-        @pl.loop(0, 6)
-        def _(j):
+        for j in range(6):
             cvt[tile256(j), :] = dot(ctx[...], cwv[:, tile256(j)]).astype(BF16).T
         pltpu.make_async_copy(cvt, cvt_hbm, loc.at[9]).start()
 
@@ -497,7 +487,7 @@
 
 def tail_kernel(o_hbm, x_hbm, ck_hbm, cvt_hbm, wo_hbm, cwq_hbm, cwo_hbm, w1_hbm, w2_hbm,
                 temb_ref, mod_ref, bo_ref, nw_ref, nb_ref, cgq_ref, out_ref,
-                o_v, x_v, ck, cvt, wo, cwq, cwo, w1, w2, vec, res, lin, act, u_b, ssq, sems, ring):
+                o_v, x_v, ck, cvt, wo, cwq, cwo, w1, w2, vec, res, lin, act, u_b, ssq, sc_s, w_s, sems, ring):
     n_ff = FF // FT
 
     def ff_copies(t, slot):
@@ -522,15 +512,13 @@
         get.start()
     get_x.wait()
 
-    @pl.loop(0, 6)
-    def _(j):
+    for j in range(6):
         cols = tile256(j)
         prod = dot(o_v[0], wo[0:HALF, cols]) + dot(o_v[1], wo[HALF:D, cols])
         res[:, cols] = x_v[:, cols].astype(F32) + vec[2:3, cols] * (prod + vec[BO:BO + 1, cols])
 
-    @pl.loop(0, TOK // 32)
-    def _(part):
-        rows = pl.ds(pl.multiple_of(part * 32, 32), 32)
+    for part in range(TOK // 32):
+        rows = slice(part * 32, (part + 1) * 32)
         act[rows] = (layer_norm_rows(res[rows]) * vec[NW:NW + 1] + vec[NB:NB + 1]).astype(BF16)
     get_cwq.wait()
     for t in range(RING):
@@ -538,8 +526,7 @@
             get.start()
     ssq[...] = jnp.zeros_like(ssq)
 
-    @pl.loop(0, 6)
-    def _(j):
+    for j in range(6):
         prod = dot(act[...], cwq[:, tile256(j)])
         lin[:, tile256(j)] = prod
         ssq[...] += fold_sq(prod)
@@ -547,26 +534,39 @@
     get_ck.wait()
     get_cvt.wait()
 
-    @pl.loop(0, HEADS // 2)
-    def _(hp):
-        for h2 in (0, 1):
-            cols = tile128(hp * 2 + h2)
-            q_h = (lin[:, cols] * q_inv * vec[CGQ:CGQ + 1, cols]).astype(BF16)
-            sc = dot_dims(ck[:, cols], q_h, 1, 1)
-            m_row = jnp.max(sc, axis=0, keepdims=True) * EXP_SCALE
-            w = jnp.exp2(sc * EXP_SCALE - m_row)
-            o_t = dot(cvt[cols, :], w.astype(BF16)) / jnp.sum(w, axis=0, keepdims=True)
-            act[:, cols] = o_t.T.astype(BF16)
+    def score(h):
+        cols = slice(h * LANES, (h + 1) * LANES)
+        q_h = (lin[:, cols] * q_inv * vec[CGQ:CGQ + 1, cols]).astype(BF16)
+        sc = dot_dims(ck[:, cols], q_h, 1, 1)
+        sc_s[h % 3] = sc
+        return jnp.max(sc, axis=0, keepdims=True) * EXP_SCALE
+
+    def weigh(h, m_row):
+        w = jnp.exp2(sc_s[h % 3] * EXP_SCALE - m_row)
+        w_s[h % 2] = w.astype(BF16)
+        return jnp.sum(w, axis=0, keepdims=True)
+
+    def finish(h, total):
+        cols = slice(h * LANES, (h + 1) * LANES)
+        act[:, cols] = (dot(cvt[cols, :], w_s[h % 2]) / total).T.astype(BF16)
+
+    m_rows = {0: score(0), 1: score(1)}
+    total = None
+    for h in range(HEADS):
+        total_prev, total = total, weigh(h, m_rows[h])
+        if h + 2 < HEADS:
+            m_rows[h + 2] = score(h + 2)
+        if h:
+            finish(h - 1, total_prev)
+    finish(HEADS - 1, total)
     get_cwo.wait()
 
-    @pl.loop(0, 6)
-    def _(j):
+    for j in range(6):
         cols = tile256(j)
         res[:, cols] += dot(act[...], cwo[:, cols])
 
-    @pl.loop(0, TOK // 32)
-    def _(part):
-        rows = pl.ds(pl.multiple_of(part * 32, 32), 32)
+    for part in range(TOK // 32):
+        rows = slice(part * 32, (part + 1) * 32)
         act[rows] = (layer_norm_rows(res[rows]) * (1.0 + vec[4:5]) + vec[3:4]).astype(BF16)
         lin[rows] = jnp.zeros((32, D), F32)
 
@@ -589,9 +589,8 @@
 
     lax.fori_loop(0, n_ff, ffn, 0)
 
-    @pl.loop(0, TOK // 32)
-    def _(part):
-        rows = pl.ds(pl.multiple_of(part * 32, 32), 32)
+    for part in range(TOK // 32):
+        rows = slice(part * 32, (part + 1) * 32)
         out_ref[0, rows] = (res[rows] + vec[5:6] * lin[rows]).astype(BF16)
 
 
@@ -608,6 +607,7 @@
             pltpu.VMEM((2, TOK, HALF), BF16), pltpu.VMEM((TOK, D), BF16), pltpu.VMEM((TEXT, D), BF16), pltpu.VMEM((D, TEXT), BF16),
             square, square, square, pltpu.VMEM((RING, D, FT), BF16), pltpu.VMEM((RING, FT, D), BF16), pltpu.VMEM((16, D), F32),
             pltpu.VMEM((TOK, D), F32), pltpu.VMEM((TOK, D), F32), pltpu.VMEM((TOK, D), BF16), pltpu.VMEM((TOK, FT), BF16), pltpu.VMEM((TOK, LANES), F32),
+            pltpu.VMEM((3, TEXT, TOK), F32), pltpu.VMEM((2, TEXT, TOK), BF16),
             pltpu.SemaphoreType.DMA((7,)), pltpu.SemaphoreType.DMA((2, RING)),
         ],
         cost_estimate=pl.CostEstimate(flops=4 * TOK * D * FF + 6 * TOK * D * D, bytes_accessed=4 * D * FF + 6 * D * D, transcendentals=TOK * FF),

time: 143 us -> 132 us (0.923)
  Pallas kernels: 142 us -> 131 us
    pallas_call x1, Pallas kernels: 40.8 us -> 31.4 us  [tail(): pl.pallas_call(tail_kernel, out_shape=jax.ShapeDtypeStruct((1, TOK, D), B...]
    pallas_call x1, Pallas kernels: 102 us -> 99.7 us  [gather_attention(): pl.pallas_call(attn_kernel, out_shape=[jax.ShapeDtypeStruct((2, TOK, HALF...]
where the time goes in v2:
time: 132 us; the launch traced here: 131 us
  Pallas kernels  131 us (99%)
    pallas_call x1, Pallas kernels, gather_attention(): pl.pallas_call(attn_kernel, out_shape=[jax.ShapeDtypeStruct((2, TOK, HALF...  99.7 us
    pallas_call x1, Pallas kernels, tail(): pl.pallas_call(tail_kernel, out_shape=jax.ShapeDtypeStruct((1, TOK, D), B...  31.4 us

profile of v2, /device:TPU:0, one launch (start us, length us, event | category | flops | bytes accessed | tf_op | source)
XLA Modules:
  0.0 131.3 jit_solution(13801742685131133625)
XLA Ops:
  0.0 99.7 %gather_attention.1 = (bf16[2,256,768]{2,1,0:T(8,128)(2,1)}, bf16[512,1536]{1,0:T(8,128)(2,1)}, bf16[1536,512]{1,0:T(8,128)(2,1)}) custom-call(bf16[1,256,1536]{2,1,0:T(8,128)(2,1)} %x_hbm.3, f32[64,256]{1,0:T(8,128)} %bitcast.7, bf16[1,512,1536]{2,1,0:T(8,128)(2,1)} %c_hbm.1, bf16[1536,1536]{1,0:T(8,128)(2,1)} %wq_hbm.1, bf16[1536,1536]{1,0:T(8,128)(2,1)} %wk_hbm.1, ...), custom_call_target="tpu_custom_call" | custom-call | flops 25769803776 | bytes 23592960 | tf_op jit(solution)/shard_map/gather_attention/pallas_call | solution.py:462
  99.7 31.4 %tail.1 = bf16[1,256,1536]{2,1,0:T(8,128)(2,1)} custom-call(bf16[2,256,768]{2,1,0:T(8,128)(2,1)} %get-tuple-element.8.o_hbm, bf16[1,256,1536]{2,1,0:T(8,128)(2,1)} %x_hbm.3, bf16[512,1536]{1,0:T(8,128)(2,1)} %get-tuple-element.9.ck_hbm, bf16[1536,512]{1,0:T(8,128)(2,1)} %get-tuple-element.10.cvt_hbm, bf16[1536,1536]{1,0:T(8,128)(2,1)} %wo_hbm.1, ...), custom_call_target="tpu_custom_call" | custom-call | flops 17716740096 | bytes 69206016 | tf_op jit(solution)/shard_map/tail/pallas_call | solution.py:601

commit v3 on v2

--- a/solution.py
+++ b/solution.py
@@ -17,7 +17,6 @@
 WIDE = 256
 TEXT = 512
 HALF = 768
-DUAL = 32
 AUX = 136
 FT = 1280
 RING = 4
@@ -111,14 +110,11 @@
     def slot_d(i):
         return z_of(i) * 4 + (1 - yy) * 2 + 1 - cc
 
-    X1, X2, DU, M1, AX = 'x1', 'x2', 'du', 'm1', 'ax'
-    rows_of = {X1: (0, LANES), X2: (LANES, LANES), DU: (0, DUAL), M1: (DUAL, LANES - DUAL)}
-    sem_of = {X1: 0, M1: 0, X2: 1, DU: 2, AX: 3}
+    X1, X2, AX = range(3)
 
     def copy(slot, part, to):
-        ref = abuf.at[slot] if part == AX else ybuf.at[slot, pl.ds(*rows_of[part])]
-        key = sem_of[part]
-        return pltpu.make_async_remote_copy(ref, ref, ss.at[to, key, slot], rs.at[key, slot], device_id=dev[to], device_id_type=MESH)
+        ref = abuf.at[slot] if part == AX else ybuf.at[slot, pl.ds(part * LANES, LANES)]
+        return pltpu.make_async_remote_copy(ref, ref, ss.at[to, part, slot], rs.at[part, slot], device_id=dev[to], device_id_type=MESH)
 
     def start(slot, to, *parts):
         for part in parts:
@@ -138,6 +134,15 @@
             act(UP)
 
         @pl.when(z > 0)
+        def _():
+            act(DN)
+
+    def leave_ends(act):
+        @pl.when(z == 0)
+        def _():
+            act(UP)
+
+        @pl.when(z == 3)
         def _():
             act(DN)
 
@@ -189,7 +194,7 @@
     def _():
         pl.semaphore_wait(barrier, 4)
 
-    start(mine, YP, DU, M1)
+    start(mine, YP, X1)
     along_z(lambda to: start(mine, to, X1))
     start(mine, CP, X1, X2)
 
@@ -231,33 +236,30 @@
     send_q = pltpu.make_async_remote_copy(q_loc.at[1 - cc], q_got, qo_s.at[0], qo_r.at[0], device_id=dev[CP], device_id_type=MESH)
     send_q.start()
 
-    peer0 = slot_b(0)
-    got(peer0, DU)
-    along_z(lambda to: start(peer0, to, DU))
-    start(peer0, CP, DU)
-
     def event_a(i, hf):
         slot = slot_a(i)
-        peer = slot_b(i)
-        if hf:
-            got(slot, X2)
-            relay(i, lambda to: start(slot, to, X2))
-            start(slot, YP, X2)
-            start(slot, CP, X2)
-        else:
-            got(slot, X1, AX)
-            relay(i, lambda to: start(slot, to, X1, AX))
-            start(slot, YP, M1, AX)
-            start(slot, CP, X1, AX)
-            got(peer, DU)
-            relay(i, lambda to: start(peer, to, DU))
-            start(peer, CP, DU)
+        parts = (X2,) if hf else (X1, AX)
+        got(slot, *parts)
+        relay(i, lambda to: start(slot, to, *parts))
+        start(slot, CP, *parts)
+        if not hf or i == 2:
+            start(slot, YP, *parts)
+        elif i == 1:
+            pl.when(ends)(lambda: start(slot, YP, *parts))
 
     def event_b(i, hf):
         slot = slot_b(i)
-        parts = (X2,) if hf else (M1, AX)
+        parts = (X2,) if hf else (X1, AX)
         got(slot, *parts)
         start(slot, CP, *parts)
+        if hf and not i:
+            leave_ends(lambda to: start(slot, to, X2))
+
+    def event_dual(i):
+        slot = slot_b(i)
+        got(slot, X2)
+        relay(i, lambda to: start(slot, to, X2))
+        start(slot, CP, X2)
 
     for h in range(6):
         cols = slice(h * LANES, (h + 1) * LANES)
@@ -298,9 +300,21 @@
             cvt[tile256(j), :] = dot(ctx[...], cwv[:, tile256(j)]).astype(BF16).T
         pltpu.make_async_copy(cvt, cvt_hbm, loc.at[9]).start()
 
-    at_ends = {2: ('a', 1, 0), 4: ('a', 1, 1), 6: ('a', 2, 0), 8: ('a', 2, 1), 10: ('a', 3, 0), 12: ('a', 3, 1)}
-    at_mids = {2: ('a', 1, 0, 2, 0), 4: ('a', 1, 1, 2, 1), 8: ('a', 3, 0), 10: ('a', 3, 1)}
-    at_all = {3: (0, 0), 5: (0, 1), 7: (1, 0), 9: (1, 1), 11: (2, 0), 13: (2, 1), 14: (3, 0), 15: (3, 1)}
+    def on(act, *args):
+        return lambda: act(*args)
+
+    at_ends = {2: [on(event_a, 1, 0)], 4: [on(event_a, 1, 1)], 6: [on(event_a, 2, 0)], 8: [on(event_a, 2, 1)],
+               9: [on(event_b, 1, 1)], 10: [on(event_a, 3, 0)], 12: [on(event_a, 3, 1)], 15: [on(event_dual, 3)]}
+    at_mids = {2: [on(event_a, 1, 0), on(event_a, 2, 0)], 4: [on(event_a, 1, 1), on(event_a, 2, 1)],
+               8: [on(event_a, 3, 0), on(event_dual, 1)], 10: [on(event_a, 3, 1)], 12: [on(event_dual, 3)]}
+    at_all = {3: [on(event_b, 0, 0)], 5: [on(event_b, 0, 1)], 7: [on(event_b, 1, 0)], 11: [on(event_b, 2, 0)],
+              13: [on(event_b, 2, 1)], 14: [on(event_b, 3, 0)]}
+
+    def run(acts):
+        def go():
+            for act in acts:
+                act()
+        return go
 
     def body(it, _):
         first = (15 - it) // 14
@@ -312,44 +326,26 @@
         hf = mid * (r // 2) + (first + last) * (it % 2)
         idx = mid * (k + 1 - r % 2) + last * 3
 
-        for step in range(16):
-            has_ends, has_mids, has_all = step in at_ends, step in at_mids, step in at_all
-            if not (has_ends or has_mids or has_all):
-                continue
-
+        for step in range(2, 16):
             @pl.when(it == step)
-            def _(step=step, has_ends=has_ends, has_mids=has_mids, has_all=has_all):
-                if has_ends:
-                    @pl.when(ends)
-                    def _():
-                        event_a(*at_ends[step][1:3])
-                if has_mids:
-                    @pl.when(mids)
-                    def _():
-                        todo = at_mids[step][1:]
-                        for n in range(0, len(todo), 2):
-                            event_a(todo[n], todo[n + 1])
-                if has_all:
-                    event_b(*at_all[step])
+            def _(step=step):
+                for where, table in ((ends, at_ends), (mids, at_mids)):
+                    if step in table:
+                        pl.when(where)(run(table[step]))
+                run(at_all.get(step, ()))()
 
         pl.when(it == 4)(cross_k)
         pl.when(it == 8)(cross_v)
 
-        @pl.when(jnp.logical_and(is_bd == 0, hf == 0))
-        def _():
-            got(slot_c(idx), X1, AX)
-
-        @pl.when(jnp.logical_and(is_bd == 0, hf == 1))
-        def _():
-            got(slot_c(idx), X2)
-
-        @pl.when(jnp.logical_and(is_bd == 1, hf == 0))
-        def _():
-            got(slot_d(idx), DU, M1, AX)
-
-        @pl.when(jnp.logical_and(is_bd == 1, hf == 1))
-        def _():
-            got(slot_d(idx), X2)
+        pair_slot = (1 - is_bd) * slot_c(idx) + is_bd * slot_d(idx)
+
+        @pl.when(hf == 0)
+        def _():
+            got(pair_slot, X1, AX)
+
+        @pl.when(hf == 1)
+        def _():
+            got(pair_slot, X2)
 
         y_of = (1 - is_bd) * yy + is_bd * (1 - yy)
         base = z_of(idx) * 4 + y_of * 2
@@ -425,27 +421,24 @@
     send_o.start()
     keep_o.start()
 
-    sent(mine, YP, DU, M1, AX, X2)
-    sent(mine, CP, X1, X2, AX)
-    sent(peer0, CP, DU)
-
-    def sent_z(to):
-        sent(mine, to, X1, AX, X2)
-        sent(peer0, to, DU)
-    along_z(sent_z)
-    for i in (1, 2, 3):
-        slot = slot_a(i)
-        peer = slot_b(i)
-
-        def sent_on(to, slot=slot, peer=peer):
-            sent(slot, to, X1, AX, X2)
-            sent(peer, to, DU)
-        relay(i, sent_on)
-        sent(slot, YP, M1, AX, X2)
-        sent(slot, CP, X1, AX, X2)
-        sent(peer, CP, DU)
+    every = (X1, X2, AX)
+    sent(mine, YP, *every)
+    sent(mine, CP, *every)
+    along_z(lambda to: sent(mine, to, *every))
+    leave_ends(lambda to: sent(slot_b(0), to, X2))
+    for i in range(1, 4):
+        relay(i, lambda to, i=i: sent(slot_a(i), to, *every))
+        sent(slot_a(i), CP, *every)
+        sent(slot_a(i), YP, X1, AX)
+    sent(slot_a(2), YP, X2)
+    pl.when(ends)(lambda: sent(slot_a(1), YP, X2))
+
+    @pl.when(mids)
+    def _():
+        for i in (1, 3):
+            relay(i, lambda to, i=i: sent(slot_b(i), to, X2))
     for i in range(4):
-        sent(slot_b(i), CP, M1, AX, X2)
+        sent(slot_b(i), CP, *every)
     send_q.wait_send()
     pltpu.make_async_copy(ck, ck_hbm, loc.at[8]).wait()
     pltpu.make_async_copy(cvt, cvt_hbm, loc.at[9]).wait()
@@ -476,7 +469,7 @@
             pltpu.VMEM((TOK, HALF), F32), pltpu.VMEM((3, TOK, 2 * TOK), F32), pltpu.VMEM((2, TOK, 2 * TOK), BF16),
             pltpu.VMEM((TEXT, D), F32), pltpu.VMEM((TEXT, D), BF16), pltpu.VMEM((D, TEXT), BF16), pltpu.VMEM((2, TOK, LANES), F32),
             pltpu.VMEM((2, TOK, HALF), BF16),
-            pltpu.SemaphoreType.DMA((4, 16)), pltpu.SemaphoreType.DMA((4, 4, 16)), pltpu.SemaphoreType.DMA((11,)),
+            pltpu.SemaphoreType.DMA((3, 16)), pltpu.SemaphoreType.DMA((4, 3, 16)), pltpu.SemaphoreType.DMA((11,)),
             pltpu.SemaphoreType.DMA((2,)), pltpu.SemaphoreType.DMA((2,)),
         ],
         cost_estimate=pl.CostEstimate(flops=2 * keys * D * D + 4 * keys * HALF * 2 * TOK, bytes_accessed=10 * D * D, transcendentals=6 * keys * 2 * TOK),

time: 132 us -> 122 us (0.924)
  Pallas kernels: 131 us -> 122 us
    pallas_call x1, Pallas kernels: 99.7 us -> 90.6 us  [gather_attention(): pl.pallas_call(attn_kernel, out_shape=[jax.ShapeDtypeStruct((2, TOK, HALF...]
where the time goes in v3:
time: 122 us
  Pallas kernels  122 us (100%)
    pallas_call x1, Pallas kernels, gather_attention(): pl.pallas_call(attn_kernel, out_shape=[jax.ShapeDtypeStruct((2, TOK, HALF...  90.6 us
    pallas_call x1, Pallas kernels, tail(): pl.pallas_call(tail_kernel, out_shape=jax.ShapeDtypeStruct((1, TOK, D), B...  31.4 us

profile of v3, /device:TPU:0, one launch (start us, length us, event | category | flops | bytes accessed | tf_op | source)
XLA Modules:
  0.0 122.2 jit_solution(2252266291381950428)
XLA Ops:
  0.0 90.6 %gather_attention.1 = (bf16[2,256,768]{2,1,0:T(8,128)(2,1)}, bf16[512,1536]{1,0:T(8,128)(2,1)}, bf16[1536,512]{1,0:T(8,128)(2,1)}) custom-call(bf16[1,256,1536]{2,1,0:T(8,128)(2,1)} %x_hbm.3, f32[64,256]{1,0:T(8,128)} %bitcast.7, bf16[1,512,1536]{2,1,0:T(8,128)(2,1)} %c_hbm.1, bf16[1536,1536]{1,0:T(8,128)(2,1)} %wq_hbm.1, bf16[1536,1536]{1,0:T(8,128)(2,1)} %wk_hbm.1, ...), custom_call_target="tpu_custom_call" | custom-call | flops 25769803776 | bytes 23592960 | tf_op jit(solution)/shard_map/gather_attention/pallas_call | solution.py:455
  90.6 31.4 %tail.1 = bf16[1,256,1536]{2,1,0:T(8,128)(2,1)} custom-call(bf16[2,256,768]{2,1,0:T(8,128)(2,1)} %get-tuple-element.8.o_hbm, bf16[1,256,1536]{2,1,0:T(8,128)(2,1)} %x_hbm.3, bf16[512,1536]{1,0:T(8,128)(2,1)} %get-tuple-element.9.ck_hbm, bf16[1536,512]{1,0:T(8,128)(2,1)} %get-tuple-element.10.cvt_hbm, bf16[1536,1536]{1,0:T(8,128)(2,1)} %wo_hbm.1, ...), custom_call_target="tpu_custom_call" | custom-call | flops 17716740096 | bytes 69206016 | tf_op jit(solution)/shard_map/tail/pallas_call | solution.py:594

commit v4 on v3

--- a/solution.py
+++ b/solution.py
@@ -304,7 +304,7 @@
         return lambda: act(*args)
 
     at_ends = {2: [on(event_a, 1, 0)], 4: [on(event_a, 1, 1)], 6: [on(event_a, 2, 0)], 8: [on(event_a, 2, 1)],
-               9: [on(event_b, 1, 1)], 10: [on(event_a, 3, 0)], 12: [on(event_a, 3, 1)], 15: [on(event_dual, 3)]}
+               9: [on(event_b, 1, 1)], 10: [on(event_a, 3, 0)], 12: [on(event_a, 3, 1)]}
     at_mids = {2: [on(event_a, 1, 0), on(event_a, 2, 0)], 4: [on(event_a, 1, 1), on(event_a, 2, 1)],
                8: [on(event_a, 3, 0), on(event_dual, 1)], 10: [on(event_a, 3, 1)], 12: [on(event_dual, 3)]}
     at_all = {3: [on(event_b, 0, 0)], 5: [on(event_b, 0, 1)], 7: [on(event_b, 1, 0)], 11: [on(event_b, 2, 0)],
@@ -333,6 +333,8 @@
                     if step in table:
                         pl.when(where)(run(table[step]))
                 run(at_all.get(step, ()))()
+                if step == 14:
+                    pl.when(ends)(on(event_dual, 3))
 
         pl.when(it == 4)(cross_k)
         pl.when(it == 8)(cross_v)
@@ -410,16 +412,19 @@
 
     lax.fori_loop(0, 16, body, 0)
 
+    def o_copies(part):
+        cols = pl.ds(part * (HALF // 2), HALF // 2)
+        away = pltpu.make_async_remote_copy(obuf.at[1 - cc, :, cols], o_hbm.at[cc, :, cols], qo_s.at[1 + part], qo_r.at[1 + part], device_id=dev[CP], device_id_type=MESH)
+        return away, pltpu.make_async_copy(obuf.at[cc, :, cols], o_hbm.at[cc, :, cols], loc.at[10 + part])
+
     for h in range(6):
         cols = slice(h * LANES, (h + 1) * LANES)
         o_h = (acc[h] / jnp.sum(l_s[h], axis=0, keepdims=True)).T.astype(BF16)
         obuf[0, :, cols] = o_h[:TOK]
         obuf[1, :, cols] = o_h[TOK:]
-    send_o = pltpu.make_async_remote_copy(obuf.at[1 - cc], o_hbm.at[cc], qo_s.at[1], qo_r.at[1], device_id=dev[CP], device_id_type=MESH)
-    got_o = pltpu.make_async_remote_copy(obuf.at[1 - cc], o_hbm.at[1 - cc], qo_s.at[1], qo_r.at[1], device_id=dev[CP], device_id_type=MESH)
-    keep_o = pltpu.make_async_copy(obuf.at[cc], o_hbm.at[cc], loc.at[10])
-    send_o.start()
-    keep_o.start()
+        if h % 3 == 2:
+            for put in o_copies(h // 3):
+                put.start()
 
     every = (X1, X2, AX)
     sent(mine, YP, *every)
@@ -442,9 +447,11 @@
     send_q.wait_send()
     pltpu.make_async_copy(ck, ck_hbm, loc.at[8]).wait()
     pltpu.make_async_copy(cvt, cvt_hbm, loc.at[9]).wait()
-    send_o.wait_send()
-    keep_o.wait()
-    got_o.wait_recv()
+    for part in (0, 1):
+        away, keep = o_copies(part)
+        away.wait_send()
+        keep.wait()
+        away.wait_recv()
 
 
 def gather_attention(*args):
@@ -469,8 +476,8 @@
             pltpu.VMEM((TOK, HALF), F32), pltpu.VMEM((3, TOK, 2 * TOK), F32), pltpu.VMEM((2, TOK, 2 * TOK), BF16),
             pltpu.VMEM((TEXT, D), F32), pltpu.VMEM((TEXT, D), BF16), pltpu.VMEM((D, TEXT), BF16), pltpu.VMEM((2, TOK, LANES), F32),
             pltpu.VMEM((2, TOK, HALF), BF16),
-            pltpu.SemaphoreType.DMA((3, 16)), pltpu.SemaphoreType.DMA((4, 3, 16)), pltpu.SemaphoreType.DMA((11,)),
-            pltpu.SemaphoreType.DMA((2,)), pltpu.SemaphoreType.DMA((2,)),
+            pltpu.SemaphoreType.DMA((3, 16)), pltpu.SemaphoreType.DMA((4, 3, 16)), pltpu.SemaphoreType.DMA((12,)),
+            pltpu.SemaphoreType.DMA((3,)), pltpu.SemaphoreType.DMA((3,)),
         ],
         cost_estimate=pl.CostEstimate(flops=2 * keys * D * D + 4 * keys * HALF * 2 * TOK, bytes_accessed=10 * D * D, transcendentals=6 * keys * 2 * TOK),
         compiler_params=pltpu.CompilerParams(collective_id=0, has_side_effects=True, vmem_limit_bytes=VMEM_MAX),
@@ -489,9 +496,13 @@
                 pltpu.make_async_copy(w2_hbm.at[cols], w2.at[slot], ring.at[1, slot]))
 
     gets = [pltpu.make_async_copy(src, dst, sems.at[n]) for n, (src, dst) in enumerate(
-        ((o_hbm, o_v), (wo_hbm, wo), (x_hbm.at[0], x_v), (cwq_hbm, cwq), (ck_hbm, ck), (cvt_hbm, cvt), (cwo_hbm, cwo)))]
-    get_o, get_wo, get_x, get_cwq, get_ck, get_cvt, get_cwo = gets
-    for get in (get_o, get_wo, get_x, get_cwq):
+        ((o_hbm, o_v), (x_hbm.at[0], x_v), (cwq_hbm, cwq), (ck_hbm, ck), (cvt_hbm, cvt), (cwo_hbm, cwo)))]
+    get_o, get_x, get_cwq, get_ck, get_cvt, get_cwo = gets
+    get_wo = []
+    for part in range(3):
+        cols = slice(part * 2 * WIDE, (part + 1) * 2 * WIDE)
+        get_wo.append(pltpu.make_async_copy(wo_hbm.at[:, cols], wo.at[:, cols], sems.at[6 + part]))
+    for get in (get_o, get_wo[0], get_x, get_wo[1], get_wo[2]):
         get.start()
     for row in range(6):
         vec[row:row + 1] = ada_row(temb_ref, mod_ref, row)
@@ -500,13 +511,14 @@
         vec[row:row + 1] = as_row(ref)
 
     get_o.wait()
-    get_wo.wait()
-    for get in (get_ck, get_cvt, get_cwo):
-        get.start()
     get_x.wait()
 
     for j in range(6):
         cols = tile256(j)
+        if j % 2 == 0:
+            get_wo[j // 2].wait()
+            for get in ((get_cwq,), (), (get_ck, get_cvt, get_cwo))[j // 2]:
+                get.start()
         prod = dot(o_v[0], wo[0:HALF, cols]) + dot(o_v[1], wo[HALF:D, cols])
         res[:, cols] = x_v[:, cols].astype(F32) + vec[2:3, cols] * (prod + vec[BO:BO + 1, cols])
 
@@ -601,7 +613,7 @@
             square, square, square, pltpu.VMEM((RING, D, FT), BF16), pltpu.VMEM((RING, FT, D), BF16), pltpu.VMEM((16, D), F32),
             pltpu.VMEM((TOK, D), F32), pltpu.VMEM((TOK, D), F32), pltpu.VMEM((TOK, D), BF16), pltpu.VMEM((TOK, FT), BF16), pltpu.VMEM((TOK, LANES), F32),
             pltpu.VMEM((3, TEXT, TOK), F32), pltpu.VMEM((2, TEXT, TOK), BF16),
-            pltpu.SemaphoreType.DMA((7,)), pltpu.SemaphoreType.DMA((2, RING)),
+            pltpu.SemaphoreType.DMA((9,)), pltpu.SemaphoreType.DMA((2, RING)),
         ],
         cost_estimate=pl.CostEstimate(flops=4 * TOK * D * FF + 6 * TOK * D * D, bytes_accessed=4 * D * FF + 6 * D * D, transcendentals=TOK * FF),
         compiler_params=pltpu.CompilerParams(vmem_limit_bytes=VMEM_MAX),

time: 122 us -> 121 us (level)
  Pallas kernels: 122 us -> 120 us
    pallas_call x1, Pallas kernels: 90.6 us -> 89.1 us  [gather_attention(): pl.pallas_call(attn_kernel, out_shape=[jax.ShapeDtypeStruct((2, TOK, HALF...]
where the time goes in v4:
time: 121 us
  Pallas kernels  120 us (99%)
    pallas_call x1, Pallas kernels, gather_attention(): pl.pallas_call(attn_kernel, out_shape=[jax.ShapeDtypeStruct((2, TOK, HALF...  89.1 us
    pallas_call x1, Pallas kernels, tail(): pl.pallas_call(tail_kernel, out_shape=jax.ShapeDtypeStruct((1, TOK, D), B...  31.3 us

profile of v4, /device:TPU:0, one launch (start us, length us, event | category | flops | bytes accessed | tf_op | source)
XLA Modules:
  0.0 120.6 jit_solution(7544788787183364502)
XLA Ops:
  0.0 89.1 %gather_attention.1 = (bf16[2,256,768]{2,1,0:T(8,128)(2,1)}, bf16[512,1536]{1,0:T(8,128)(2,1)}, bf16[1536,512]{1,0:T(8,128)(2,1)}) custom-call(bf16[1,256,1536]{2,1,0:T(8,128)(2,1)} %x_hbm.3, f32[64,256]{1,0:T(8,128)} %bitcast.7, bf16[1,512,1536]{2,1,0:T(8,128)(2,1)} %c_hbm.1, bf16[1536,1536]{1,0:T(8,128)(2,1)} %wq_hbm.1, bf16[1536,1536]{1,0:T(8,128)(2,1)} %wk_hbm.1, ...), custom_call_target="tpu_custom_call" | custom-call | flops 25769803776 | bytes 23592960 | tf_op jit(solution)/shard_map/gather_attention/pallas_call | solution.py:462
  89.1 31.3 %tail.1 = bf16[1,256,1536]{2,1,0:T(8,128)(2,1)} custom-call(bf16[2,256,768]{2,1,0:T(8,128)(2,1)} %get-tuple-element.8.o_hbm, bf16[1,256,1536]{2,1,0:T(8,128)(2,1)} %x_hbm.3, bf16[512,1536]{1,0:T(8,128)(2,1)} %get-tuple-element.9.ck_hbm, bf16[1536,512]{1,0:T(8,128)(2,1)} %get-tuple-element.10.cvt_hbm, bf16[1536,1536]{1,0:T(8,128)(2,1)} %wo_hbm.1, ...), custom_call_target="tpu_custom_call" | custom-call | flops 17716740096 | bytes 69206016 | tf_op jit(solution)/shard_map/tail/pallas_call | solution.py:606
